TPU v7x, 32 devices: a whole 2x2x4 slice. The times are simulated.
32 devices in a mesh: pair: 8 (over z, x), aux: 4 (over y, core).
Axes of the slice: x: 2, y: 2, z: 4, core: 2. Of those that a mesh axis runs over, the one named last changes fastest.
Arguments:
- panels: bfloat16 [16, 120, 9216], P('pair', None, 'aux'), may hold values from -1.5 to 1.5
- amplitudes: bfloat16 [16, 2, 120, 120], P('pair'), may hold values from -0.5 to 0.5
- drive: float32 [16, 2, 14400], P('pair', None, 'aux'), may hold values from -6 to 6
- pno_energy: float32 [16, 120], P('pair'), may hold values from 1 to 3
- occ_energy: float32 [32], replicated, may hold values from -2 to -0.5
- frequency: float32 [1], replicated, may hold values from 0.2 to 2
- pair_lmo: int32 [16, 2], replicated, may hold values from 0 to 31
- neighbours: int32 [16, 8], P('pair'), may hold values from 0 to 15
- pno_ranks: int32 [16], P('pair'), may hold values from 60 to 120
- fock_off: float32 [32, 32], replicated, may hold values from -1.8 to 1.8
Outputs:
- residual: float32 [16, 2, 14400], P('pair', None, 'aux')
Inputs may be any that keep to these rules, and one draw needn't show every extreme that they name: `neighbours`: neighbour pairs; a pair may be listed more than once and may list itself. `pno_ranks`: rows of a pair's panel from its rank on are padding.
All inputs are finite; a program needn't handle non-finite values.
Results may differ from a plain program's by a relative error of at most 0.0033.
Values may be sent and summed in bfloat16 or wider, within the bound.
No kernel may reach another device: no remote copies, remote signals or barrier semaphores. Data moves between devices by JAX's collectives and lax.ppermute only.
A program may use at most 128 MiB of HBM per device.

v0:
```python
import math

import jax
import jax.numpy as jnp
from jax import lax
from jax.sharding import PartitionSpec as P


def pair_weights(pair_lmo, neighbours, fock_off, first_pair):
    local_pairs = neighbours.shape[0]
    total_pairs = pair_lmo.shape[0]
    lmo_count = fock_off.shape[0]
    lmo_ids = jnp.arange(lmo_count, dtype=jnp.int32)
    own_lmo = lax.dynamic_slice_in_dim(pair_lmo, first_pair, local_pairs, 0)
    own_table = (own_lmo[:, :, None] == lmo_ids[None, None, :]).astype(jnp.float32)
    lmo_table = (pair_lmo[:, :, None] == lmo_ids[None, None, :]).astype(jnp.float32)
    pair_ids = jnp.arange(total_pairs, dtype=jnp.int32)
    onehot = (neighbours[:, :, None] == pair_ids[None, None, :]).astype(jnp.float32)
    fock_rows = jnp.einsum("psl,lm->psm", own_table, fock_off, precision=lax.Precision.HIGHEST)
    near_table = jnp.einsum("pkn,nsl->pksl", onehot, lmo_table)
    values = jnp.sum(fock_rows[:, None, :, :] * near_table, axis=(2, 3))
    weights = jnp.sum(values[:, :, None] * onehot, axis=1).astype(jnp.bfloat16)
    return (weights, own_table)


def project_pairs(slab, amp_block):
    group_size = slab.shape[0]
    matrices = jnp.transpose(amp_block, (0, 2, 1, 3)).reshape(group_size, amp_block.shape[2], -1)
    return jnp.einsum("nra,nrc->nac", slab, matrices, preferred_element_type=jnp.float32).astype(
        jnp.bfloat16
    )


def accumulate(weights, group_limit, running_sum, arriving):
    slab_rows, amp_rows = arriving
    pair_count = slab_rows.shape[0]
    group_size = math.gcd(pair_count, group_limit)

    def group_turn(turn_index, partial_sum):
        offset = turn_index * group_size
        slab = lax.dynamic_slice_in_dim(slab_rows, offset, group_size, 0)
        amp_block = lax.dynamic_slice_in_dim(amp_rows, offset, group_size, 0)
        projected = project_pairs(slab, amp_block)
        coeff_block = lax.dynamic_slice_in_dim(weights, offset, group_size, 1)
        return partial_sum + jnp.einsum(
            "pn,nac->pac", coeff_block, projected, preferred_element_type=jnp.float32
        )

    return lax.fori_loop(0, pair_count // group_size, group_turn, running_sum)


def close_coupling(masked, collected_sum, freq_count):
    local_pairs, rank_dim, aux_width = masked.shape
    collected = collected_sum.astype(jnp.bfloat16)
    coupled = jnp.einsum("pra,pac->prc", masked, collected, preferred_element_type=jnp.float32)
    coupled = jnp.transpose(
        coupled.reshape(local_pairs, rank_dim, freq_count, rank_dim), (0, 2, 1, 3)
    )
    return coupled.reshape(local_pairs, freq_count, rank_dim * rank_dim)


def body(
    panels,
    amplitudes,
    drive,
    pno_energy,
    occ_energy,
    frequency,
    pair_lmo,
    neighbours,
    pno_ranks,
    fock_off,
):
    local_pairs, rank_dim, aux_width = panels.shape
    first_pair = lax.axis_index("pair") * local_pairs
    rows_index = jnp.arange(rank_dim, dtype=jnp.int32)
    keep_rows = rows_index[None, :] < pno_ranks[:, None]
    masked = jnp.where(keep_rows[:, :, None], panels, jnp.zeros_like(panels))
    weights, own_table = pair_weights(pair_lmo, neighbours, fock_off, first_pair)
    start_sum = jnp.zeros((local_pairs, aux_width, 2 * rank_dim), jnp.float32)
    collected_sum = accumulate(
        weights,
        4,
        start_sum,
        (
            lax.all_gather(masked, "pair", axis=0, tiled=True),
            lax.all_gather(amplitudes, "pair", axis=0, tiled=True),
        ),
    )
    coupled_terms = close_coupling(masked, collected_sum, 2)
    coupled_share = lax.psum_scatter(coupled_terms, "aux", scatter_dimension=2, tiled=True)
    share_width = drive.shape[2]
    share_start = lax.axis_index("aux") * share_width
    occ_pair = jnp.sum(own_table * occ_energy[None, None, :], axis=(1, 2))
    shift = pno_energy[:, :, None] + pno_energy[:, None, :] - occ_pair[:, None, None]
    shift_flat = lax.dynamic_slice_in_dim(
        shift.reshape(local_pairs, rank_dim * rank_dim), share_start, share_width, 1
    )
    signs = jnp.array([1.0, -1.0], jnp.float32)
    factor = shift_flat[:, None, :] - signs[None, :, None] * frequency[0]
    amp_flat = amplitudes.reshape(local_pairs, 2, rank_dim * rank_dim)
    amp_share = lax.dynamic_slice_in_dim(amp_flat, share_start, share_width, 2).astype(jnp.float32)
    return drive + factor * amp_share + coupled_share


def solution(mesh):
    placed = (
        P("pair", None, "aux"),
        P("pair", None, None, None),
        P("pair", None, "aux"),
        P("pair", None),
        P(),
        P(),
        P(),
        P("pair", None),
        P("pair"),
        P(),
    )
    return jax.shard_map(
        body, mesh=mesh, in_specs=placed, out_specs=P("pair", None, "aux"), check_vma=False
    )
```

profile of v0, /device:TPU:0, one launch (start us, length us, event | category | flops | bytes accessed | tf_op | source)
XLA Modules:
  0.0 319.1 jit_solution(4289958824527709440)
XLA Ops:
  6.5 0.0 copy-start
  6.5 0.0 all-gather.2.cloned.1.call-start
  6.5 0.7 iota_compare_fusion.4
  7.3 2.4 broadcast_select_fusion
  9.7 0.0 all-gather.2.cloned.1.call-update
  9.7 0.0 reduce-scatter.4.cloned.1.call-start
  9.8 0.8 constant_dynamic-slice_fusion.2
  10.5 0.1 copy.22
  10.6 0.8 broadcast_add_fusion
  11.5 0.2 add.67
  11.7 0.8 select_reduce_fusion.1
  12.5 0.0 copy-done
  12.5 0.2 fusion.8
  12.7 1.0 fusion.7
  13.7 0.8 select_reduce_fusion
  14.5 39.0 %all_gather.7 = bf16[16,2,120,120]{3,2,1,0:T(8,128)(2,1)S(1)} all-gather(bf16[2,2,120,120]{3,2,1,0:T(8,128)(2,1)} %param.14), channel_id=1, replica_groups=mesh['pair'=8,'aux'=4] {'pair'}, dimensions={0}, use_global_device_ids=true | all-gather | bytes 1036800 | tf_op jit(solution)/shard_map/all_gather | solution.py:87
  53.5 97.1 %all-gather.2.cloned.1.call-done = bf16[16,120,2304]{2,1,0:T(8,128)(2,1)} async-done(((bf16[2,120,2304]{2,1,0:T(8,128)(2,1)}), bf16[16,120,2304]{2,1,0:T(8,128)(2,1)}) %all-gather.2.cloned.1.call-update) | async-done | bytes 8847376 | tf_op jit(solution)/shard_map/all_gather | solution.py:86
  150.5 55.8 %while.14 = (s32[]{:T(128)}, f32[2,2304,240]{1,0,2:T(2,128)}, bf16[2,16]{1,0:T(2,128)(2,1)S(1)}, bf16[16,120,2304]{2,1,0:T(8,128)(2,1)}, bf16[16,2,120,120]{3,2,...) while((s32[]{:T(128)}, f32[2,2304,240]{1,0,2:T(2,128)}, ...), condition=%wide.region_4.5_spmd.clone, body=%wide.region_3.4_spmd.clone.sunk | while | flops 544112640 | bytes 21058792 | solution.py:49
  150.6 0.2 copy.39
  150.7 5.0 %convolution_convert_fusion.2 = bf16[4,2304,240]{1,2,0:T(8,128)(2,1)} fusion(bf16[4,120,240]{1,2,0:T(8,128)(2,1)S(1)} %bitcast.35, bf16[16,120,2304]{2,1,0:T(8,128)(2,1)} %get-tuple-element.185, s32[]{:T(128)S(6)} %select_n.26), kind=kOutput, calls=%fused_computation.clone.1 | convolution fusion | flops 533053440 | bytes 6865924 | tf_op jit(solution)/shard_map/while/body/eval_jaxpr/nra,nrc->nac/dot_general | solution.py:29
  155.8 7.7 %convolution_add_fusion.2 = f32[2,2304,240]{1,0,2:T(2,128)} fusion(f32[2,2304,240]{1,0,2:T(2,128)} %get-tuple-element.174, bf16[4,2304,240]{1,2,0:T(8,128)(2,1)} %convolution_convert_fusion.2, pred[]{:T(512)S(6)} %compare.3, bf16[2,16]{1,0:T(2,128)(2,1)S(1)} %get-tuple-element.184, s32[]{:T(128)S(6)} %select_n.26), kind=kOutput, calls=%fused_computation.1.clone.1 | convolution fusion | flops 11059200 | bytes 13271109 | tf_op jit(solution)/shard_map/while/body/eval_jaxpr/pn,nac->pac/dot_general | solution.py:45
  163.5 0.2 copy.39
  163.7 5.0 %convolution_convert_fusion.2 = bf16[4,2304,240]{1,2,0:T(8,128)(2,1)} fusion(bf16[4,120,240]{1,2,0:T(8,128)(2,1)S(1)} %bitcast.35, bf16[16,120,2304]{2,1,0:T(8,128)(2,1)} %get-tuple-element.185, s32[]{:T(128)S(6)} %select_n.26), kind=kOutput, calls=%fused_computation.clone.1 | convolution fusion | flops 533053440 | bytes 6865924 | tf_op jit(solution)/shard_map/while/body/eval_jaxpr/nra,nrc->nac/dot_general | solution.py:29
  168.7 9.1 %convolution_add_fusion.2 = f32[2,2304,240]{1,0,2:T(2,128)} fusion(f32[2,2304,240]{1,0,2:T(2,128)} %get-tuple-element.174, bf16[4,2304,240]{1,2,0:T(8,128)(2,1)} %convolution_convert_fusion.2, pred[]{:T(512)S(6)} %compare.3, bf16[2,16]{1,0:T(2,128)(2,1)S(1)} %get-tuple-element.184, s32[]{:T(128)S(6)} %select_n.26), kind=kOutput, calls=%fused_computation.1.clone.1 | convolution fusion | flops 11059200 | bytes 13271109 | tf_op jit(solution)/shard_map/while/body/eval_jaxpr/pn,nac->pac/dot_general | solution.py:45
  177.8 0.2 copy.39
  178.0 5.0 %convolution_convert_fusion.2 = bf16[4,2304,240]{1,2,0:T(8,128)(2,1)} fusion(bf16[4,120,240]{1,2,0:T(8,128)(2,1)S(1)} %bitcast.35, bf16[16,120,2304]{2,1,0:T(8,128)(2,1)} %get-tuple-element.185, s32[]{:T(128)S(6)} %select_n.26), kind=kOutput, calls=%fused_computation.clone.1 | convolution fusion | flops 533053440 | bytes 6865924 | tf_op jit(solution)/shard_map/while/body/eval_jaxpr/nra,nrc->nac/dot_general | solution.py:29
  183.0 9.1 %convolution_add_fusion.2 = f32[2,2304,240]{1,0,2:T(2,128)} fusion(f32[2,2304,240]{1,0,2:T(2,128)} %get-tuple-element.174, bf16[4,2304,240]{1,2,0:T(8,128)(2,1)} %convolution_convert_fusion.2, pred[]{:T(512)S(6)} %compare.3, bf16[2,16]{1,0:T(2,128)(2,1)S(1)} %get-tuple-element.184, s32[]{:T(128)S(6)} %select_n.26), kind=kOutput, calls=%fused_computation.1.clone.1 | convolution fusion | flops 11059200 | bytes 13271109 | tf_op jit(solution)/shard_map/while/body/eval_jaxpr/pn,nac->pac/dot_general | solution.py:45
  192.1 0.2 copy.39
  192.2 5.0 %convolution_convert_fusion.2 = bf16[4,2304,240]{1,2,0:T(8,128)(2,1)} fusion(bf16[4,120,240]{1,2,0:T(8,128)(2,1)S(1)} %bitcast.35, bf16[16,120,2304]{2,1,0:T(8,128)(2,1)} %get-tuple-element.185, s32[]{:T(128)S(6)} %select_n.26), kind=kOutput, calls=%fused_computation.clone.1 | convolution fusion | flops 533053440 | bytes 6865924 | tf_op jit(solution)/shard_map/while/body/eval_jaxpr/nra,nrc->nac/dot_general | solution.py:29
  197.3 9.1 %convolution_add_fusion.2 = f32[2,2304,240]{1,0,2:T(2,128)} fusion(f32[2,2304,240]{1,0,2:T(2,128)} %get-tuple-element.174, bf16[4,2304,240]{1,2,0:T(8,128)(2,1)} %convolution_convert_fusion.2, pred[]{:T(512)S(6)} %compare.3, bf16[2,16]{1,0:T(2,128)(2,1)S(1)} %get-tuple-element.184, s32[]{:T(128)S(6)} %select_n.26), kind=kOutput, calls=%fused_computation.1.clone.1 | convolution fusion | flops 11059200 | bytes 13271109 | tf_op jit(solution)/shard_map/while/body/eval_jaxpr/pn,nac->pac/dot_general | solution.py:45
  206.3 0.0 copy-start.1
  206.3 3.9 %convert_element_type.21 = bf16[2,2304,240]{1,0,2:T(2,128)(2,1)S(1)} convert(f32[2,2304,240]{1,0,2:T(2,128)} %get-tuple-element.99) | non-fusion elementwise | flops 1105920 | bytes 6635520 | tf_op jit(solution)/shard_map/convert_element_type | solution.py:54
  210.2 0.0 copy-done.1
  210.2 0.9 fusion.5
  211.1 0.2 reshape.54
  211.3 12.1 %copy.29 = f32[2,2,120,120]{1,0,3,2:T(2,128)} copy(f32[2,2,120,120]{3,1,2,0:T(2,128)S(1)} %bitcast.37) | data formatting | bytes 460800
  223.3 14.5 %reshape.61 = f32[14400,4]{1,0:T(8,128)} reshape(f32[14400,2,2]{2,1,0:T(2,128)} %bitcast.34) | data formatting | bytes 460800
  237.9 0.0 reduce-scatter.4.cloned.1.call-update
  237.9 0.1 dynamic-slice_subtract_fusion
  238.0 0.8 copy-done.2
  238.8 0.3 reshape.53
  239.8 0.0 copy-done.4
  239.8 0.0 copy-start.3
  239.8 62.6 %reduce-scatter.4.cloned.1.call-done = f32[3600,4]{1,0:T(8,128)} async-done(((f32[14400,4]{1,0:T(8,128)}), f32[3600,4]{1,0:T(8,128)}) %reduce-scatter.4.cloned.1.call-update) | async-done | bytes 57616
  302.5 4.9 %reshape.62 = f32[3600,2,2]{2,1,0:T(2,128)} reshape(f32[3600,4]{1,0:T(8,128)} %reduce-scatter.4.cloned.1.call-done) | data formatting | bytes 115200
  307.3 4.2 %copy.28 = f32[2,2,3600]{2,1,0:T(2,128)S(1)} copy(f32[2,2,3600]{1,0,2:T(2,128)} %bitcast.36) | data formatting | bytes 115200
  311.5 0.0 copy-done.3
  311.5 0.7 add_add_fusion
  (8 shorter events, 0.1 us)
Async XLA Ops:
  6.5 6.0 %copy-start = (f32[32,32]{1,0:T(8,128)S(1)}, f32[32,32]{1,0:T(8,128)}, u32[]{:S(2)}) copy-start(f32[32,32]{1,0:T(8,128)} %param.22) | copy-start | bytes 12292
  6.5 144.0 %all-gather.2.cloned.1.call-start = ((), (), s32[]{:S(2)}) async-start(), calls=%async_computation.1 | async-start | bytes 9953280 | tf_op jit(solution)/shard_map/all_gather | solution.py:86
  9.7 292.7 %reduce-scatter.4.cloned.1.call-start = ((), (), s32[]{:S(2)}) async-start(), calls=%async_computation.2 | async-start | bytes 9216000
  206.3 3.9 %copy-start.1 = (bf16[2,120,2304]{2,1,0:T(8,128)(2,1)S(1)}, bf16[2,120,2304]{2,1,0:T(8,128)(2,1)}, u32[]{:S(2)}) copy-start(bf16[2,120,2304]{2,1,0:T(8,128)(2,1)} %broadcast_select_fusion) | copy-start | bytes 3317764
  237.9 0.9 copy-start.2
  237.9 1.9 copy-start.4
  239.8 71.7 %copy-start.3 = (f32[2,2,3600]{2,1,0:T(2,128)S(1)}, f32[2,2,3600]{2,1,0:T(2,128)}, u32[]{:S(2)}) copy-start(f32[2,2,3600]{2,1,0:T(2,128)} %param.15) | copy-start | bytes 172804
Sparse Core Ops, SparseCore 0:
  9.8 140.6 all-gather.1
  238.0 64.3 reduce-scatter.3
where the time goes:
time: 320 us; the launch traced here: 319 us
  waiting for transfers between devices  160 us (50%)
  matrix products  57 us (18%)
  blocking collectives  39 us (12%)
  local copies, waits for them, and re-layouts  38.8 us (12%)
  between operations  14.2 us (4%)
  other arithmetic  10.3 us (3%)
    all_gather x1, waiting for transfers between devices, body(): lax.all_gather(masked, 'pair', axis=0, tiled=True)  97.1 us
    unnamed x3, waiting for transfers between devices  62.7 us
    all_gather x1, blocking collectives, body(): lax.all_gather(amplitudes, 'pair', axis=0, tiled=True)  39 us
    unnamed x14, local copies, waits for them, and re-layouts  36.5 us
    dot_general x4, matrix products, group_turn(): jnp.einsum('pn,nac->pac', coeff_block, projected, preferred_element_type=...  34.9 us
    dot_general x4, matrix products, project_pairs(): jnp.einsum('nra,nrc->nac', slab, matrices, preferred_element_type=jnp.flo...  20.1 us
  transfers between devices with their start and end apart: 2, of which 2 were waited for; matrix products, arithmetic and copies ran while one was open for 2% of the time, Pallas kernels for 0%

commit v1 on v0

v1 whole, which is shorter than its diff:
```python
import functools

import jax
import jax.numpy as jnp
from jax import lax
from jax.experimental import pallas as pl
from jax.experimental.pallas import tpu as pltpu
from jax.sharding import PartitionSpec as P

LANES = 128
BF = jnp.bfloat16
F32 = jnp.float32


def round_up(value, unit):
    return -(-value // unit) * unit


def pair_weights(pair_lmo, neighbours, fock_off, first_pair):
    local_pairs = neighbours.shape[0]
    total_pairs = pair_lmo.shape[0]
    lmo_count = fock_off.shape[0]
    lmo_ids = jnp.arange(lmo_count, dtype=jnp.int32)
    own_lmo = lax.dynamic_slice_in_dim(pair_lmo, first_pair, local_pairs, 0)
    own_table = (own_lmo[:, :, None] == lmo_ids[None, None, :]).astype(F32)
    lmo_table = (pair_lmo[:, :, None] == lmo_ids[None, None, :]).astype(F32)
    pair_ids = jnp.arange(total_pairs, dtype=jnp.int32)
    onehot = (neighbours[:, :, None] == pair_ids[None, None, :]).astype(F32)
    fock_rows = jnp.einsum("psl,lm->psm", own_table, fock_off, precision=lax.Precision.HIGHEST)
    near_table = jnp.einsum("pkn,nsl->pksl", onehot, lmo_table)
    values = jnp.sum(fock_rows[:, None, :, :] * near_table, axis=(2, 3))
    weights = jnp.sum(values[:, :, None] * onehot, axis=1).astype(BF)
    return (weights, own_table)


def couple_kernel(blocks, aux_ref, w_ref, x_ref, a_ref, out_ref, proj_ref):
    total, width, depth = x_ref.shape
    freqs = a_ref.shape[1]
    lanes = a_ref.shape[3]
    local = out_ref.shape[3]
    rows = depth // blocks
    my_core = aux_ref[0] % 2

    def project(n, carry):
        x = x_ref[n]
        for s in range(freqs):
            proj_ref[n, :, s * lanes : (s + 1) * lanes] = jnp.dot(
                x, a_ref[n, s], preferred_element_type=F32
            )
        return carry

    lax.fori_loop(0, total, project, 0)

    def close(p, carry):
        acc = w_ref[p, 0] * proj_ref[0]
        for n in range(1, total):
            acc = acc + w_ref[p, n] * proj_ref[n]
        got = lax.dot_general(
            x_ref[p], acc.astype(BF), (((0,), (0,)), ((), ())), preferred_element_type=F32
        )
        for h in range(blocks):
            side = (my_core + h) % 2 if blocks > 1 else 0
            for s in range(freqs):
                out_ref[side, p // local, h // 2, p % local, s] = got[
                    h * rows : (h + 1) * rows, s * lanes : (s + 1) * lanes
                ].astype(out_ref.dtype)
        return carry

    lax.fori_loop(0, total, close, 0)


def body(sizes, panels, amplitudes, drive, pno_energy, occ_energy, frequency, pair_lmo,
         neighbours, pno_ranks, fock_off):
    n_pair, n_aux = sizes
    local, rank, width = panels.shape
    freqs = amplitudes.shape[1]
    total = pair_lmo.shape[0]
    even = rank % n_aux == 0 and n_aux % 2 == 0
    blocks = n_aux if even else 1
    rows = rank // blocks
    rows_pad = round_up(rows, 16)
    depth = round_up(blocks * rows_pad, LANES)
    rows_pad = depth // blocks
    part = width // n_pair
    me_pair = lax.axis_index("pair")
    me_aux = lax.axis_index("aux")

    weights, own_table = pair_weights(pair_lmo, neighbours, fock_off, me_pair * local)

    keep = jnp.arange(rank, dtype=jnp.int32)[None, :] < pno_ranks[:, None]
    masked = jnp.where(keep[:, :, None], panels, jnp.zeros_like(panels))
    spread = jnp.pad(
        masked.reshape(local, blocks, rows, width), ((0, 0), (0, 0), (0, rows_pad - rows), (0, 0))
    ).reshape(local, depth, n_pair, part)
    spread = jnp.transpose(spread, (2, 0, 3, 1)).reshape(n_pair, local * part, depth)
    amp = jnp.pad(
        amplitudes.reshape(local, freqs, blocks, rows, rank),
        ((0, 0), (0, 0), (0, 0), (0, rows_pad - rows), (0, LANES - rank)),
    ).reshape(n_aux, -1, LANES)
    amp_rows = amp.shape[1]
    share = lax.dynamic_index_in_dim(amp, me_aux, 0, keepdims=False)
    tail = jnp.pad(weights, ((0, 16 - local), (0, LANES - total)))
    extra = jnp.concatenate([share, tail], axis=0)
    sent = jnp.concatenate(
        [spread, jnp.broadcast_to(extra[None], (n_pair,) + extra.shape)], axis=1
    )
    got = lax.all_to_all(sent, "pair", 0, 0, tiled=True)
    xt = got[:, : local * part].reshape(total, part, depth)
    w_all = got[:, local * part + amp_rows :][:, :local, :total].reshape(total, total).astype(F32)
    mats = got[:, local * part : local * part + amp_rows][None]
    step = n_aux // 2
    while step >= 1:
        other = lax.ppermute(mats, "aux", [(i, i ^ step) for i in range(n_aux)])
        mats = jnp.concatenate([mats, other], axis=0)
        step //= 2
    order = []
    for member in range(n_aux):
        j, bit, step = 0, 1, n_aux // 2
        slot = jnp.int32(0)
        while step >= 1:
            slot = slot + bit * (((me_aux ^ member) & step) > 0).astype(jnp.int32)
            bit, step = bit * 2, step // 2
        order.append(lax.dynamic_index_in_dim(mats, slot, 0, keepdims=False))
    mats = jnp.stack(order, axis=1).reshape(total, freqs, depth, LANES)

    out_dims = (2 if even else 1, n_pair, max(blocks // 2, 1), local, freqs, rows_pad, LANES)
    vmem = pl.BlockSpec(memory_space=pltpu.VMEM)
    smem = pl.BlockSpec(memory_space=pltpu.SMEM)
    flops = 4 * total * part * depth * freqs * LANES
    coupled = pl.pallas_call(
        functools.partial(couple_kernel, blocks),
        out_shape=jax.ShapeDtypeStruct(out_dims, BF if even else F32),
        in_specs=[smem, smem, vmem, vmem],
        out_specs=vmem,
        scratch_shapes=[pltpu.VMEM((total, part, freqs * LANES), F32)],
        compiler_params=pltpu.CompilerParams(vmem_limit_bytes=40 * 2**20),
        cost_estimate=pl.CostEstimate(flops=flops, bytes_accessed=4 * 2**20, transcendentals=0),
    )(me_aux.reshape(1), w_all, xt, mats)

    if even:
        other = lax.ppermute(coupled[1], "aux", [(i, i ^ 1) for i in range(n_aux)])
        mine = (coupled[0].astype(F32) + other.astype(F32)).astype(BF)
        mine = mine.reshape((n_pair * (n_aux // 2),) + out_dims[3:])
        groups = [
            [g * n_aux + 2 * h + c for g in range(n_pair) for h in range(n_aux // 2)]
            for c in range(2)
        ]
        parts = lax.all_to_all(
            mine, ("pair", "aux"), 0, 0, axis_index_groups=groups, tiled=True
        )
        coupled_share = jnp.sum(parts.astype(F32), axis=0)[:, :, :rows, :rank].reshape(
            local, freqs, rows * rank
        )
    else:
        flat = coupled.reshape(total, freqs, depth, LANES)[:, :, :rank, :rank]
        flat = flat.reshape(total, freqs, rank * rank)
        share_aux = lax.psum_scatter(flat, "aux", scatter_dimension=2, tiled=True)
        coupled_share = lax.psum_scatter(share_aux, "pair", scatter_dimension=0, tiled=True)

    share_width = drive.shape[2]
    start = me_aux * share_width
    occ_pair = jnp.sum(own_table * occ_energy[None, None, :], axis=(1, 2))
    shift = pno_energy[:, :, None] + pno_energy[:, None, :] - occ_pair[:, None, None]
    signs = jnp.array([1.0, -1.0], F32)
    if even:
        energy_rows = lax.dynamic_slice_in_dim(pno_energy, me_aux * rows, rows, 1)
        shift = energy_rows[:, :, None] + pno_energy[:, None, :] - occ_pair[:, None, None]
        factor = shift[:, None] - signs[None, :, None, None] * frequency[0]
        amp_rows_own = lax.dynamic_slice_in_dim(amplitudes, me_aux * rows, rows, 2)
        diagonal = (factor * amp_rows_own.astype(F32)).reshape(local, freqs, share_width)
    else:
        factor = shift[:, None] - signs[None, :, None, None] * frequency[0]
        diagonal = (factor * amplitudes.astype(F32)).reshape(local, freqs, rank * rank)
        diagonal = lax.dynamic_slice_in_dim(diagonal, start, share_width, 2)
    return drive + diagonal + coupled_share


def solution(mesh):
    placed = (
        P("pair", None, "aux"),
        P("pair", None, None, None),
        P("pair", None, "aux"),
        P("pair", None),
        P(),
        P(),
        P(),
        P("pair", None),
        P("pair"),
        P(),
    )
    sizes = (mesh.shape["pair"], mesh.shape["aux"])
    return jax.shard_map(
        functools.partial(body, sizes),
        mesh=mesh,
        in_specs=placed,
        out_specs=P("pair", None, "aux"),
        check_vma=False,
    )
```

time: 320 us -> 98.8 us (0.31)
  waiting for transfers between devices: 160 us -> 21.8 us
  matrix products: 57 us -> 1.18 us
  local copies, waits for them, and re-layouts: 38.8 us -> 7.15 us
  between operations: 14.2 us -> 0.92 us
  Pallas kernels: 0 us -> 11 us
  starting transfers between devices: 0.04 us -> 8.06 us
  other arithmetic: 10.3 us -> 6.12 us
  blocking collectives: 39 us -> 42.2 us
    all_gather x1 -> x0, waiting for transfers between devices: 97.1 us -> none  [body(): lax.all_gather(masked, 'pair', axis=0, tiled=True)]
    unnamed x3 -> x0, waiting for transfers between devices: 62.7 us -> none
    dot_general x9 -> x0, matrix products: 55.9 us -> none  [the longest x4 34.9 us: group_turn(): jnp.einsum('pn,nac->pac', coeff_block, projected, preferred_element_type=...]
    all_to_all x0 -> x1, blocking collectives: none -> 42.2 us  [body(): got = lax.all_to_all(sent, 'pair', 0, 0, tiled=True)]
    all_gather x1 -> x0, blocking collectives: 39 us -> none  [body(): lax.all_gather(amplitudes, 'pair', axis=0, tiled=True)]
    unnamed x14 -> x13, local copies, waits for them, and re-layouts: 36.5 us -> 1.16 us
    all_to_all x0 -> x1, waiting for transfers between devices: none -> 13.4 us  [body(): lax.all_to_all(mine, ('pair', 'aux'), 0, 0, axis_index_groups=groups, til...]
    pallas_call x0 -> x1, Pallas kernels: none -> 11 us  [body(): pl.pallas_call(functools.partial(couple_kernel, blocks), out_shape=jax.Sh...]
  transfers between devices with their start and end apart: 2 -> 4, of which waited for: 2 -> 4; matrix products, arithmetic and copies ran while one was open for 2% -> 1% of each run, Pallas kernels for 0% -> 0%
where the time goes in v1:
time: 98.8 us; the launch traced here: 98.3 us
  blocking collectives  42.2 us (43%)
  waiting for transfers between devices  21.8 us (22%)
  Pallas kernels  11 us (11%)
  starting transfers between devices  8.06 us (8%)
  local copies, waits for them, and re-layouts  7.15 us (7%)
  other arithmetic  6.12 us (6%)
  matrix products  1.18 us (1%)
    all_to_all x1, blocking collectives, body(): got = lax.all_to_all(sent, 'pair', 0, 0, tiled=True)  42.2 us
    all_to_all x1, waiting for transfers between devices, body(): lax.all_to_all(mine, ('pair', 'aux'), 0, 0, axis_index_groups=groups, til...  13.4 us
    pallas_call x1, Pallas kernels, body(): pl.pallas_call(functools.partial(couple_kernel, blocks), out_shape=jax.Sh...  11 us
    ppermute x2, waiting for transfers between devices, body(): other = lax.ppermute(mats, 'aux', [(i, i ^ step) for i in range(n_aux)])  6.71 us
    all_to_all x1, starting transfers between devices, body(): lax.all_to_all(mine, ('pair', 'aux'), 0, 0, axis_index_groups=groups, til...  6.07 us
    reshape x1, local copies, waits for them, and re-layouts, body(): spread = jnp.pad(masked.reshape(local, blocks, rows, width), ((0, 0), (0,...  2.45 us
  transfers between devices with their start and end apart: 4, of which 4 were waited for; matrix products, arithmetic and copies ran while one was open for 1% of the time, Pallas kernels for 0%

profile of v1, /device:TPU:0, one launch (start us, length us, event | category | flops | bytes accessed | tf_op | source)
XLA Modules:
  0.0 98.3 jit_solution(4255874600110702013)
XLA Ops:
  0.0 0.0 copy-start
  0.0 0.8 constant_dynamic-slice_fusion
  0.8 0.1 copy.18
  0.9 0.0 copy-done
  0.9 0.2 fusion.4
  1.1 1.0 fusion
  2.0 0.8 select_reduce_fusion
  2.8 1.0 %copy.22 = bf16[2,2,120,120]{3,1,2,0:T(2,128)(2,1)S(1)} copy(bf16[2,2,120,120]{3,2,1,0:T(8,128)(2,1)} %param.12) | data formatting | bytes 230400 | tf_op args[1]
  3.8 0.7 iota_compare_fusion.5
  4.6 1.4 %broadcast_select_fusion = bf16[2,120,2304]{2,1,0:T(8,128)(2,1)S(1)} fusion(bf16[2,120,2304]{2,1,0:T(8,128)(2,1)} %param.11, pred[2,120]{1,0:T(4,128)(4,1)S(1)} %iota_compare_fusion.5), kind=kLoop, calls=%fused_computation.3 | loop fusion | flops 552960 | bytes 2212080 | tf_op jit(solution)/shard_map/jit(_where)/select_n | solution.py:91
  6.0 0.9 copy.19
  6.8 0.1 copy.25
  7.0 0.1 pad.12.clone
  7.1 2.5 %reshape.80 = bf16[2,128,8,288]{3,2,1,0:T(8,128)(2,1)S(1)} reshape(bf16[2,4,32,2304]{3,2,1,0:T(8,128)(2,1)S(1)} %pad.12.clone) | data formatting | bytes 2359296 | tf_op jit(solution)/shard_map/reshape | solution.py:94
  9.5 1.1 %copy.21 = bf16[8,2,288,128]{3,2,1,0:T(8,128)(2,1)S(1)} copy(bf16[8,2,288,128]{2,0,3,1:T(8,128)(2,1)S(1)} %bitcast.48) | data formatting | bytes 2359296 | tf_op jit(solution)/shard_map/transpose | solution.py:95
  10.7 0.1 pad_maximum_fusion
  10.8 42.2 %all_to_all.10 = bf16[8,720,128]{2,1,0:T(8,128)(2,1)S(1)} all-to-all(bf16[8,720,128]{2,1,0:T(8,128)(2,1)S(1)} %pad_maximum_fusion), channel_id=1, replica_groups=mesh['pair'=8,'aux'=4] {'pair'}, dimensions={0} | all-to-all | bytes 2949120 | tf_op jit(solution)/shard_map/all_to_all | solution.py:107
  53.0 1.6 %collective-permute-start = (bf16[1,8,128,128]{3,2,1,0:T(8,128)(2,1)S(1)}, bf16[1,8,128,128]{3,2,1,0:T(8,128)(2,1)S(1)}, u32[]{:S(2)}, u32[]{:S(2)}) collective-permute-start(bf16[1,8,128,128]{3,2,1,0:T(8,128)(2,1)S(1)} %slice_bitcast_fusion.2), channel_id=1, source_target_pairs={{0,2},{1,3},{2,0},{3,1},{4,6},{5,7},{6,4},{7,5},{8,10},{9,11},{10,... | collective-permute-start | bytes 786440 | tf_op jit(solution)/shard_map/ppermute | solution.py:113
  54.6 5.0 %collective-permute-done = bf16[1,8,128,128]{3,2,1,0:T(8,128)(2,1)S(1)} collective-permute-done((bf16[1,8,128,128]{3,2,1,0:T(8,128)(2,1)S(1)}, bf16[1,8,128,128]{3,2,1,0:T(8,128)(2,1)S(1)}, u32[]{:S(2)}, u32[]{:S(2)}) %collective-permute-start) | collective-permute-done | bytes 262176 | tf_op jit(solution)/shard_map/ppermute | solution.py:113
  59.5 0.1 pad_maximum_fusion.3
  59.6 0.1 collective-permute-start.1
  59.7 0.1 slice.27
  59.8 1.7 %collective-permute-done.1 = bf16[2,8,128,128]{3,2,1,0:T(8,128)(2,1)S(1)} collective-permute-done((bf16[2,8,128,128]{3,2,1,0:T(8,128)(2,1)S(1)}, bf16[2,8,128,128]{3,2,1,0:T(8,128)(2,1)S(1)}, u32[]{:S(2)}, u32[]{:S(2)}) %collective-permute-start.1) | collective-permute-done | bytes 524320 | tf_op jit(solution)/shard_map/ppermute | solution.py:113
  61.6 0.1 pad_maximum_fusion.1
  61.7 0.1 dynamic-slice_bitcast_fusion.3
  61.8 0.1 pad_maximum_fusion.2
  61.9 11.0 %shard_map.109 = bf16[2,8,2,2,2,32,128]{6,5,4,3,2,1,0:T(8,128)(2,1)S(1)} custom-call(s32[1]{0:T(128)} %bitcast.1.aux_ref, f32[16,16]{1,0:T(8,128)S(1)} %convert.2.w_ref, bf16[16,288,128]{2,1,0:T(8,128)(2,1)S(1)} %bitcast.46, bf16[16,2,128,128]{3,2,1,0:T(8,128)(2,1)S(1)} %bitcast.47), custom_call_target="tpu_custom_call" | custom-call | flops 603979776 | bytes 4194304 | tf_op jit(solution)/shard_map/pallas_call | solution.py:130
  73.0 0.0 copy-start.2
  73.0 0.0 copy-start.3
  73.0 0.0 copy-start.4
  73.0 0.3 collective-permute-start.2
  73.3 1.6 %collective-permute-done.2 = bf16[8,2,2,2,32,128]{5,4,3,2,1,0:T(8,128)(2,1)S(1)} collective-permute-done((bf16[8,2,2,2,32,128]{5,4,3,2,1,0:T(8,128)(2,1)S(1)}, bf16[8,2,2,2,32,128]{5,4,3,2,1,0:T(8,128)(2,1)S(1)}, u32[]{:S(2)}, u32[]{:S(2)}) %collective-permute-start.2) | collective-permute-done | bytes 524320 | tf_op jit(solution)/shard_map/ppermute | solution.py:141
  75.0 1.0 %fusion.1 = bf16[8,2,2,2,32,128]{5,4,3,2,1,0:T(8,128)(2,1)} fusion(bf16[8,2,2,2,32,128]{5,4,3,2,1,0:T(8,128)(2,1)S(1)} %collective-permute-done.2, bf16[2,8,2,2,2,32,128]{6,5,4,3,2,1,0:T(8,128)(2,1)S(1)} %shard_map.109), kind=kLoop, calls=%fused_computation.7 | loop fusion | flops 1048576 | bytes 1572864 | tf_op jit(solution)/shard_map/convert_element_type | solution.py:142
  76.0 0.0 copy-start.1
  76.0 6.1 %all-to-all-start.1 = ((bf16[16,2,2,32,128]{4,3,2,1,0:T(8,128)(2,1)}), bf16[16,2,2,32,128]{4,3,2,1,0:T(8,128)(2,1)S(1)}, u32[]{:S(2)}, u32[]{:S(2)}) async-start(bf16[16,2,2,32,128]{4,3,2,1,0:T(8,128)(2,1)} %bitcast.22), calls=%async_computation.1 | async-start | bytes 1048576 | tf_op jit(solution)/shard_map/all_to_all | solution.py:148
  82.7 0.0 copy-done.2
  82.7 0.1 constant_dynamic-slice_fusion.1
  82.8 0.0 copy-done.3
  82.8 0.2 select_reduce_fusion.1
  83.0 0.0 copy-done.4
  83.0 0.1 add_subtract_fusion
  83.0 0.9 convert_multiply_fusion
  83.9 0.1 reshape.77
  84.0 13.4 %all-to-all-done.1 = bf16[16,2,2,32,128]{4,3,2,1,0:T(8,128)(2,1)S(1)} async-done(((bf16[16,2,2,32,128]{4,3,2,1,0:T(8,128)(2,1)}), bf16[16,2,2,32,128]{4,3,2,1,0:T(8,128)(2,1)S(1)}, u32[]{:S(2)}, u32[]{:S(2)}) %all-to-all-start.1) | async-done | bytes 524320 | tf_op jit(solution)/shard_map/all_to_all | solution.py:148
  97.4 0.1 convert_reduce_fusion
  97.5 0.1 reshape.87
  97.6 0.0 copy-done.1
  97.6 0.7 add_add_fusion
  (10 shorter events, 0.2 us)
Async XLA Ops:
  0.0 0.9 copy-start
  53.0 6.5 %collective-permute-start = (bf16[1,8,128,128]{3,2,1,0:T(8,128)(2,1)S(1)}, bf16[1,8,128,128]{3,2,1,0:T(8,128)(2,1)S(1)}, u32[]{:S(2)}, u32[]{:S(2)}) collective-permute-start(bf16[1,8,128,128]{3,2,1,0:T(8,128)(2,1)S(1)} %slice_bitcast_fusion.2), channel_id=1, source_target_pairs={{0,2},{1,3},{2,0},{3,1},{4,6},{5,7},{6,4},{7,5},{8,10},{9,11},{10,... | collective-permute-start | bytes 786440 | tf_op jit(solution)/shard_map/ppermute | solution.py:113
  59.6 2.0 %collective-permute-start.1 = (bf16[2,8,128,128]{3,2,1,0:T(8,128)(2,1)S(1)}, bf16[2,8,128,128]{3,2,1,0:T(8,128)(2,1)S(1)}, u32[]{:S(2)}, u32[]{:S(2)}) collective-permute-start(bf16[2,8,128,128]{3,2,1,0:T(8,128)(2,1)S(1)} %pad_maximum_fusion.3), channel_id=1, source_target_pairs={{0,1},{1,0},{2,3},{3,2},{4,5},{5,4},{6,7},{7,6},{8,9},{9,8},{10,11... | collective-permute-start | bytes 1572872 | tf_op jit(solution)/shard_map/ppermute | solution.py:113
  73.0 9.7 %copy-start.2 = (f32[2,120]{1,0:T(2,128)S(1)}, f32[2,120]{1,0:T(2,128)}, u32[]{:S(2)}) copy-start(f32[2,120]{1,0:T(2,128)} %param.14) | copy-start | bytes 2884
  73.0 9.8 %copy-start.3 = (f32[32]{0:T(128)S(1)}, f32[32]{0:T(128)}, u32[]{:S(2)}) copy-start(f32[32]{0:T(128)} %param.15) | copy-start | bytes 388
  73.0 10.0 %copy-start.4 = (f32[2]{0:T(128)S(1)}, f32[2]{0:T(128)}, u32[]{:S(2)}) copy-start(f32[2]{0:T(128)} %constant.51.clone) | copy-start | bytes 28
  73.0 2.0 %collective-permute-start.2 = (bf16[8,2,2,2,32,128]{5,4,3,2,1,0:T(8,128)(2,1)S(1)}, bf16[8,2,2,2,32,128]{5,4,3,2,1,0:T(8,128)(2,1)S(1)}, u32[]{:S(2)}, u32[]{:S(2)}) collective-permute-start(bf16[8,2,2,2,32,128]{5,4,3,2,1,0:T(8,128)(2,1)S(1)} %slice_bitcast_fusion), channel_id=1, source_target_pairs={{0,1},{1,0},{2,3},{3,2},{4,5},{5,4},{6,7},{7,6},{8,9},{9,8},{10,11... | collective-permute-start | bytes 1572872 | tf_op jit(solution)/shard_map/ppermute | solution.py:141
  76.0 21.7 %copy-start.1 = (f32[2,2,3600]{2,1,0:T(2,128)S(1)}, f32[2,2,3600]{2,1,0:T(2,128)}, u32[]{:S(2)}) copy-start(f32[2,2,3600]{2,1,0:T(2,128)} %param.13) | copy-start | bytes 172804
  76.0 21.5 %all-to-all-start.1 = ((bf16[16,2,2,32,128]{4,3,2,1,0:T(8,128)(2,1)}), bf16[16,2,2,32,128]{4,3,2,1,0:T(8,128)(2,1)S(1)}, u32[]{:S(2)}, u32[]{:S(2)}) async-start(bf16[16,2,2,32,128]{4,3,2,1,0:T(8,128)(2,1)} %bitcast.22), calls=%async_computation.1 | async-start | bytes 1048576 | tf_op jit(solution)/shard_map/all_to_all | solution.py:148
